TPU v7x, 32 devices: a whole 2x2x4 slice. The times are simulated.
32 devices in a mesh: rep: 8 (over y, x, core), tp: 4 (over z).
Axes of the slice: x: 2, y: 2, z: 4, core: 2. Of those that a mesh axis runs over, the one named last changes fastest.
Arguments:
- queries: bfloat16 [256, 4096], P('rep', 'tp'), may hold values from -110 to 110
- new_key_value: bfloat16 [256, 4, 256], P('rep', 'tp'), may hold values from -6 to 6
- key_value_cache: bfloat16 [256, 4, 128, 256], P('rep', 'tp'), may hold values from -4 to 4
- lengths: int32 [256], P('rep'), may hold values from 2 to 128
- residual: bfloat16 [256, 4096], P('rep', 'tp'), may hold values from -1.1953125 to 1.1953125
- output_weight: bfloat16 [4096, 4096], P('tp'), may hold values from -0.09375 to 0.09375
- row_adapter_index: int32 [256], P('rep'), may hold values from 0 to 31, as said below
- adapter_storage_slot: int32 [32], replicated, may hold values from 0 to 31, as said below
- adapter_down_weight: bfloat16 [32, 4096, 64], P('rep', 'tp'), may hold values from -0.09375 to 0.09375
- adapter_up_weight: bfloat16 [32, 64, 4096], P('rep', None, 'tp'), may hold values from -0.75 to 0.75
Outputs:
- layer_out: bfloat16 [256, 4096], P('rep', 'tp')
Inputs may be any that keep to these rules, and one draw needn't show every extreme that they name: adapter_storage_slot holds each of 0 to 31 once. `row_adapter_index`: within the 32 rows of one index of rep, at most 16 rows use adapters with the same adapter_storage_slot // 4, and in every such block some value of it is used by exactly 16 rows.
All inputs are finite; a program needn't handle non-finite values.
Results may differ from a plain program's by a relative error of at most 0.0085.
Values may be sent and summed in bfloat16 or wider, within the bound.
A program may use at most 64 MiB of HBM per device.

v0:
```python
import functools
import math

import jax
import jax.numpy as jnp
from jax import lax
from jax.experimental import pallas as pl
from jax.experimental.pallas import tpu as pltpu
from jax.sharding import PartitionSpec as P

HEAD_WIDTH = 128
LANES = 128
F32 = jnp.float32
BF16 = jnp.bfloat16
I32 = jnp.int32
MESH = pl.DeviceIdType.MESH


def iota(shape, dim):
    return lax.broadcasted_iota(I32, shape, dim)


def as_column(row, n):
    eye = iota((n, n), 0) == iota((n, n), 1)
    return jnp.sum(jnp.where(eye, row, 0), axis=1, keepdims=True)


def as_row(col, n):
    eye = iota((n, n), 0) == iota((n, n), 1)
    return jnp.sum(jnp.where(eye, col, 0), axis=0, keepdims=True)


def divide(x, by):
    if by & (by - 1) == 0:
        return lax.shift_right_logical(x, jnp.full_like(x, by.bit_length() - 1))
    return lax.div(x, jnp.full_like(x, by))


def merge(ref, lanes=None):
    n, cap, f = ref.shape
    lo, hi = lanes if lanes else (0, f)
    if cap % 16 == 0:
        return ref[:, :, lo:hi].reshape(n * cap, hi - lo)
    return jnp.concatenate([ref[i, :, lo:hi].astype(F32) for i in range(n)], axis=0).astype(ref.dtype)


def kernel(
    n_rep, n_tp, cap, chunk, adapters,
    len_hbm, q_hbm, kv_hbm, fresh_hbm, idx_hbm, table_hbm, down_hbm, w_hbm, up_hbm, res_hbm,
    out_ref,
    len_s, q_v, kv_v, fresh_v, idx_v, table_v, down_v, w_v, up_v, res_v,
    ext_v, feat_send, feat_recv, part_send, part_recv, base_v, rs_send, rs_recv,
    ret_send, ret_recv,
    in_sem, kv_sem, w_sem,
    fs_sem, fr_sem, ps_sem, pr_sem, ss_sem, sr_sem, rs_sem, rr_sem,
):
    rep = lax.axis_index("rep")
    tp = lax.axis_index("tp")
    rows, width = q_v.shape
    heads = width // HEAD_WIDTH
    context = kv_v.shape[1]
    joined = down_v.shape[0]
    rank = joined // adapters
    out_width = up_v.shape[1]
    slots = n_rep * cap

    loads = {}
    for i, (name, src, dst) in enumerate((
        ("len", len_hbm, len_s), ("q", q_hbm, q_v), ("fresh", fresh_hbm, fresh_v),
        ("idx", idx_hbm, idx_v), ("table", table_hbm, table_v),
        ("down", down_hbm, down_v), ("up", up_hbm, up_v), ("res", res_hbm, res_v),
    )):
        loads[name] = pltpu.make_async_copy(src, dst, in_sem.at[i])
    kv_loads = [
        pltpu.make_async_copy(
            kv_hbm.at[pl.ds(c, chunk)], kv_v.at[pl.ds(c, chunk)], kv_sem.at[c // chunk]
        )
        for c in range(0, rows, chunk)
    ]
    w_loads = []
    for k in range(n_tp):
        t = lax.rem(tp + k, n_tp)
        columns = pl.ds(pl.multiple_of(t * out_width, out_width), out_width)
        w_loads.append(pltpu.make_async_copy(w_hbm.at[:, columns], w_v.at[k], w_sem.at[k]))
    for name in ("len", "q", "fresh", "idx", "table"):
        loads[name].start()
    for copy in kv_loads:
        copy.start()

    barrier = pltpu.get_barrier_semaphore()
    for k in range(1, n_rep):
        pl.semaphore_signal(
            barrier, inc=1, device_id={"rep": lax.rem(rep + k, n_rep)}, device_id_type=MESH
        )
    for k in range(1, n_tp):
        pl.semaphore_signal(
            barrier, inc=1, device_id={"tp": lax.rem(tp + k, n_tp)}, device_id_type=MESH
        )

    loads["idx"].wait()
    loads["table"].wait()
    table_size = table_v.shape[1]
    idx_col = as_column(idx_v[...], rows)
    slot_col = jnp.sum(
        jnp.where(iota((rows, table_size), 1) == idx_col, table_v[...], 0), axis=1, keepdims=True
    )
    owner_col = divide(slot_col, adapters)
    local_col = slot_col - owner_col * adapters
    owner_row = as_row(owner_col, rows)
    earlier = (owner_col == owner_row) & (iota((rows, rows), 0) < iota((rows, rows), 1))
    rank_row = jnp.sum(jnp.where(earlier, 1, 0), axis=0, keepdims=True)
    target_row = owner_row * cap + rank_row
    target_col = as_column(target_row, rows)
    place = jnp.where(iota((slots, rows), 0) == target_row, 1.0, 0.0).astype(BF16)
    place_back = jnp.where(iota((rows, slots), 1) == target_col, 1.0, 0.0).astype(BF16)
    ext_v[:, width:] = jnp.broadcast_to((local_col + 1).astype(F32), (rows, LANES)).astype(BF16)

    loads["len"].wait()
    loads["q"].wait()
    loads["fresh"].wait()
    scale = 1.0 / math.sqrt(HEAD_WIDTH)
    for c in range(0, rows, chunk):
        q = q_v[c : c + chunk, :].astype(F32).reshape(chunk, heads, HEAD_WIDTH)
        fresh = fresh_v[c : c + chunk, :].astype(F32).reshape(chunk, 1, 2 * HEAD_WIDTH)
        own = jnp.sum(q * fresh[:, :, :HEAD_WIDTH], axis=-1, keepdims=True) * scale
        live = jnp.concatenate(
            [iota((1, heads, context), 2) < len_s[c + i] for i in range(chunk)], axis=0
        )
        kv_loads[c // chunk].wait()
        if c == 0:
            for k in list(range(1, n_tp)) + [0]:
                w_loads[k].start()
            for name in ("down", "up", "res"):
                loads[name].start()
        kv = kv_v[c : c + chunk]
        scores = (
            jnp.einsum(
                "rhd,rcd->rhc", q.astype(BF16), kv[:, :, :HEAD_WIDTH], preferred_element_type=F32
            )
            * scale
        )
        scores = jnp.where(live, scores, -1e30)
        top = jnp.maximum(jnp.max(scores, axis=-1, keepdims=True), own)
        weights = jnp.where(live, jnp.exp(scores - top), 0.0)
        own_weight = jnp.exp(own - top)
        inverse = 1.0 / (jnp.sum(weights, axis=-1, keepdims=True) + own_weight)
        probs = (weights * inverse).astype(BF16)
        own_prob = (own_weight * inverse).astype(BF16).astype(F32)
        mixed = jnp.einsum(
            "rhc,rcd->rhd", probs, kv[:, :, HEAD_WIDTH:], preferred_element_type=F32
        )
        mixed = mixed + own_prob * fresh[:, :, HEAD_WIDTH:]
        ext_v[c : c + chunk, :width] = mixed.reshape(chunk, width).astype(BF16)

    outgoing = jnp.dot(place, ext_v[...], preferred_element_type=F32)
    for d in range(n_rep):
        feat_send[d] = outgoing[d * cap : (d + 1) * cap].astype(BF16)

    pl.semaphore_wait(barrier, n_rep - 1 + n_tp - 1)

    def exchange(axis, me, n, src_of, dst, send_sem, recv_sem):
        copies = []
        for k in range(1, n):
            d = lax.rem(me + k, n)
            copies.append(
                pltpu.make_async_remote_copy(
                    src_ref=src_of(k, d), dst_ref=dst(k, me), send_sem=send_sem.at[k],
                    recv_sem=recv_sem.at[k], device_id={axis: d}, device_id_type=MESH,
                )
            )
        return copies

    dispatch = exchange(
        "rep", rep, n_rep, lambda k, d: feat_send.at[d], lambda k, me: feat_recv.at[me],
        fs_sem, fr_sem,
    )
    for copy in dispatch:
        copy.start()
    feat_recv[rep] = feat_send[rep]

    reduce = exchange(
        "tp", tp, n_tp, lambda k, d: rs_send.at[k], lambda k, me: rs_recv.at[k], ss_sem, sr_sem
    )
    tile = math.gcd(out_width, 256)
    early = n_tp // 2

    def project(k):
        w_loads[k].wait()

        @pl.loop(0, out_width // tile)
        def _(j):
            columns = pl.ds(pl.multiple_of(j * tile, tile), tile)
            part = jnp.dot(ext_v[:, :width], w_v[k, :, columns], preferred_element_type=F32)
            if k == 0:
                base_v[:, columns] = part
            else:
                rs_send[k, :, columns] = part.astype(BF16)

    for k in list(range(1, n_tp)) + [0]:
        project(k)
        if 0 < k <= early:
            reduce[k - 1].start()

    for copy in dispatch:
        copy.wait_recv()

    features = merge(feat_recv, (0, width))
    tags = merge(feat_recv, (width, width + LANES)).astype(F32)
    loads["down"].wait()
    products = lax.dot_general(
        features, down_v[...], (((1,), (1,)), ((), ())), preferred_element_type=F32
    )
    tag_wide = jnp.concatenate([tags] * (joined // LANES), axis=1)
    lane_of = divide(iota((slots, joined), 1), rank) + 1
    mine = tag_wide == lane_of.astype(F32)
    masked = jnp.where(mine, products, 0.0)
    half = masked[:, :LANES]
    for b in range(1, joined // LANES):
        half = half + masked[:, b * LANES : (b + 1) * LANES]
    low = iota((slots // 2, LANES), 1) < rank
    half = half + pltpu.roll(half, rank, 1)
    packed = jnp.where(low, half[: slots // 2], half[slots // 2 :])
    part_send[...] = packed.astype(BF16)
    shrink_exchange = exchange(
        "tp", tp, n_tp, lambda k, d: part_send, lambda k, me: part_recv.at[k], ps_sem, pr_sem
    )
    for copy in shrink_exchange:
        copy.start()
    for copy in reduce[early:]:
        copy.start()
    for k, copy in enumerate(shrink_exchange):
        copy.wait_recv()
        packed = packed + part_recv[k + 1].astype(F32)

    rolled = pltpu.roll(packed, rank, 1)
    both = jnp.concatenate(
        [jnp.where(low, packed, rolled), jnp.where(low, rolled, packed)], axis=0
    )
    wide = jnp.concatenate([both] * (joined // LANES), axis=1)
    shrink = jnp.where(mine, wide, 0.0).astype(BF16)
    loads["up"].wait()
    answers = jnp.dot(shrink, up_v[...], preferred_element_type=F32)
    for d in range(n_rep):
        ret_send[d] = answers[d * cap : (d + 1) * cap].astype(BF16)
    returns = exchange(
        "rep", rep, n_rep, lambda k, d: ret_send.at[d], lambda k, me: ret_recv.at[me],
        rs_sem, rr_sem,
    )
    for copy in returns:
        copy.start()
    ret_recv[rep] = ret_send[rep]

    loads["res"].wait()
    total = res_v[...].astype(F32) + base_v[...]
    for k, copy in enumerate(reduce):
        copy.wait_recv()
        total = total + rs_recv[k + 1].astype(F32)
    for copy in returns:
        copy.wait_recv()
    update = jnp.dot(place_back, merge(ret_recv), preferred_element_type=F32)
    out_ref[...] = (total + update).astype(BF16)
    for copy in dispatch + shrink_exchange + reduce + returns:
        copy.wait_send()


def on_device(
    n_rep, n_tp, queries, new_key_value, key_value_cache, lengths, residual, output_weight,
    row_adapter_index, adapter_storage_slot, adapter_down_weight, adapter_up_weight,
):
    rows, width = queries.shape
    context = key_value_cache.shape[2]
    adapters, _, rank = adapter_down_weight.shape
    out_width = adapter_up_weight.shape[2]
    table = adapter_storage_slot.shape[0]
    cap = max(2, 4 * rows // n_rep)
    slots = n_rep * cap
    chunk = 16
    assert 2 * rank == LANES and (adapters * rank) % LANES == 0
    vmem = pltpu.VMEM
    dma = pltpu.SemaphoreType.DMA
    any_spec = pl.BlockSpec(memory_space=pl.ANY)
    return pl.pallas_call(
        functools.partial(kernel, n_rep, n_tp, cap, chunk, adapters),
        out_shape=jax.ShapeDtypeStruct((rows, out_width), BF16),
        in_specs=[any_spec] * 10,
        out_specs=pl.BlockSpec(memory_space=pltpu.VMEM),
        scratch_shapes=[
            pltpu.SMEM((rows,), I32),
            vmem((rows, width), BF16),
            vmem((rows, context, 2 * HEAD_WIDTH), BF16),
            vmem((rows, 2 * HEAD_WIDTH), BF16),
            vmem((1, rows), I32),
            vmem((1, table), I32),
            vmem((adapters * rank, width), BF16),
            vmem((n_tp, width, out_width), BF16),
            vmem((adapters * rank, out_width), BF16),
            vmem((rows, out_width), BF16),
            vmem((rows, width + LANES), BF16),
            vmem((n_rep, cap, width + LANES), BF16),
            vmem((n_rep, cap, width + LANES), BF16),
            vmem((slots // 2, LANES), BF16),
            vmem((n_tp, slots // 2, LANES), BF16),
            vmem((rows, out_width), F32),
            vmem((n_tp, rows, out_width), BF16),
            vmem((n_tp, rows, out_width), BF16),
            vmem((n_rep, cap, out_width), BF16),
            vmem((n_rep, cap, out_width), BF16),
            dma((8,)),
            dma((rows // chunk,)),
            dma((n_tp,)),
            dma((n_rep,)), dma((n_rep,)),
            dma((n_tp,)), dma((n_tp,)),
            dma((n_tp,)), dma((n_tp,)),
            dma((n_rep,)), dma((n_rep,)),
        ],
        compiler_params=pltpu.CompilerParams(collective_id=0, has_side_effects=True),
        name="layer",
    )(
        lengths, queries, key_value_cache.reshape(rows, context, 2 * HEAD_WIDTH),
        new_key_value.reshape(rows, 2 * HEAD_WIDTH), row_adapter_index.reshape(1, rows),
        adapter_storage_slot.reshape(1, table),
        jnp.swapaxes(adapter_down_weight, 1, 2).reshape(adapters * rank, width), output_weight,
        adapter_up_weight.reshape(adapters * rank, out_width), residual,
    )


def solution(mesh):
    in_specs = (
        P("rep", "tp"),
        P("rep", "tp", None),
        P("rep", "tp", None, None),
        P("rep"),
        P("rep", "tp"),
        P("tp", None),
        P("rep"),
        P(),
        P("rep", "tp", None),
        P("rep", None, "tp"),
    )
    return jax.shard_map(
        functools.partial(on_device, mesh.shape["rep"], mesh.shape["tp"]),
        mesh=mesh, in_specs=in_specs, out_specs=P("rep", "tp"), check_vma=False,
    )
```

profile of v0, /device:TPU:0, one launch (start us, length us, event | category | flops | bytes accessed | tf_op | source)
XLA Modules:
  0.0 22.7 jit_solution(17600483348453257465)
XLA Ops:
  0.0 21.2 %layer.1 = bf16[32,1024]{1,0:T(8,128)(2,1)} custom-call(s32[32]{0:T(128)} %len_hbm.1, bf16[32,1024]{1,0:T(8,128)(2,1)} %q_hbm.1, bf16[32,128,256]{2,1,0:T(8,128)(2,1)} %bitcast.8, bf16[32,256]{1,0:T(8,128)(2,1)} %bitcast.11, s32[1,32]{1,0:T(1,128)} %bitcast.12, s32[1,32]{1,0:T(1,128)} %bitcast.13, bf16[256,1024]{1,0:T(8,128)(2,1)} %bitcast.9, ...), custom_call_target="tpu_custom_call" | custom-call | tf_op jit(solution)/shard_map/layer/pallas_call | solution.py:282
  21.3 1.5 %copy.12 = bf16[32,1024]{1,0:T(8,128)(2,1)} copy(bf16[32,1024]{1,0:T(8,128)(2,1)} %layer.1) | data formatting | bytes 131072
where the time goes:
time: 22.9 us; the launch traced here: 22.7 us
  Pallas kernels  21.2 us (93%)
  local copies, waits for them, and re-layouts  1.47 us (6%)
    pallas_call x1, Pallas kernels, on_device(): pl.pallas_call(functools.partial(kernel, n_rep, n_tp, cap, chunk, adapter...  21.2 us
    unnamed x1, local copies, waits for them, and re-layouts  1.47 us

commit v1 on v0

--- a/solution.py
+++ b/solution.py
@@ -278,7 +278,7 @@
     assert 2 * rank == LANES and (adapters * rank) % LANES == 0
     vmem = pltpu.VMEM
     dma = pltpu.SemaphoreType.DMA
-    any_spec = pl.BlockSpec(memory_space=pl.ANY)
+    any_spec = pl.BlockSpec(memory_space=pltpu.HBM)
     return pl.pallas_call(
         functools.partial(kernel, n_rep, n_tp, cap, chunk, adapters),
         out_shape=jax.ShapeDtypeStruct((rows, out_width), BF16),
@@ -313,15 +313,15 @@
             dma((n_tp,)), dma((n_tp,)),
             dma((n_rep,)), dma((n_rep,)),
         ],
-        compiler_params=pltpu.CompilerParams(collective_id=0, has_side_effects=True),
+        compiler_params=pltpu.CompilerParams(collective_id=0, has_side_effects=True, vmem_limit_bytes=24 * 1024 * 1024),
         name="layer",
-    )(
+    )(*[pltpu.with_memory_space_constraint(a, pltpu.HBM) for a in (
         lengths, queries, key_value_cache.reshape(rows, context, 2 * HEAD_WIDTH),
         new_key_value.reshape(rows, 2 * HEAD_WIDTH), row_adapter_index.reshape(1, rows),
         adapter_storage_slot.reshape(1, table),
         jnp.swapaxes(adapter_down_weight, 1, 2).reshape(adapters * rank, width), output_weight,
         adapter_up_weight.reshape(adapters * rank, out_width), residual,
-    )
+    )])
 
 
 def solution(mesh):

time: 22.9 us -> 21.4 us (0.934)
  local copies, waits for them, and re-layouts: 1.47 us -> 0.63 us
  Pallas kernels: 21.2 us -> 20.6 us
    unnamed x1, local copies, waits for them, and re-layouts: 1.47 us -> 0.63 us
    pallas_call x1, Pallas kernels: 21.2 us -> 20.6 us  [on_device(): pl.pallas_call(functools.partial(kernel, n_rep, n_tp, cap, chunk, adapter...]
where the time goes in v1:
time: 21.4 us; the launch traced here: 21.3 us
  Pallas kernels  20.6 us (96%)
  local copies, waits for them, and re-layouts  0.63 us (3%)
    pallas_call x1, Pallas kernels, on_device(): pl.pallas_call(functools.partial(kernel, n_rep, n_tp, cap, chunk, adapter...  20.6 us
    unnamed x1, local copies, waits for them, and re-layouts  0.63 us

profile of v1, /device:TPU:0, one launch (start us, length us, event | category | flops | bytes accessed | tf_op | source)
XLA Modules:
  0.0 21.3 jit_solution(14845381057900742242)
XLA Ops:
  0.0 20.6 %layer.1 = bf16[32,1024]{1,0:T(8,128)(2,1)S(1)} custom-call(s32[32]{0:T(128)} %len_hbm.1, bf16[32,1024]{1,0:T(8,128)(2,1)} %q_hbm.1, bf16[32,128,256]{2,1,0:T(8,128)(2,1)} %bitcast.8, bf16[32,256]{1,0:T(8,128)(2,1)} %bitcast.11, s32[1,32]{1,0:T(1,128)} %bitcast.12, s32[1,32]{1,0:T(1,128)} %bitcast.13, bf16[256,1024]{1,0:T(8,128)(2,1)} %bitcast.9, ...), custom_call_target="tpu_custom_call" | custom-call | tf_op jit(solution)/shard_map/layer/pallas_call | solution.py:282
  20.6 0.6 %copy.12 = bf16[32,1024]{1,0:T(8,128)(2,1)} copy(bf16[32,1024]{1,0:T(8,128)(2,1)S(1)} %layer.1) | data formatting | bytes 131072

commit v2 on v1

v2 whole, which is shorter than its diff:
```python
import functools
import math

import jax
import jax.numpy as jnp
from jax import lax
from jax.experimental import pallas as pl
from jax.experimental.pallas import tpu as pltpu
from jax.sharding import PartitionSpec as P

HEAD_WIDTH = 128
LANES = 128
F32 = jnp.float32
BF16 = jnp.bfloat16
I32 = jnp.int32
MESH = pl.DeviceIdType.MESH


def iota(shape, dim):
    return lax.broadcasted_iota(I32, shape, dim)


def as_column(row, n):
    eye = iota((n, n), 0) == iota((n, n), 1)
    return jnp.sum(jnp.where(eye, row, 0), axis=1, keepdims=True)


def divide(x, by):
    if by & (by - 1) == 0:
        return lax.shift_right_logical(x, jnp.full_like(x, by.bit_length() - 1))
    return lax.div(x, jnp.full_like(x, by))


def peer(me, n, k):
    if n != 4:
        return lax.rem(me + k, n)
    return (me, me + 1 - 2 * lax.rem(me, 2), lax.rem(me + 2, 4), 3 - me)[k]


def source(me, n, k):
    return peer(me, n, k) if n == 4 else lax.rem(me + n - k, n)


def attend(q, keys, values):
    chunk, heads, _ = q.shape
    if heads % 8 or chunk % 2:
        scores = jnp.einsum("rhd,rcd->rhc", q.astype(BF16), keys, preferred_element_type=F32)
        return scores, lambda probs: jnp.einsum(
            "rhc,rcd->rhd", probs, values, preferred_element_type=F32
        )
    pairs, context = chunk // 2, keys.shape[1]
    both = (pairs, 2 * heads, HEAD_WIDTH)
    first = iota(both, 1) < heads

    def side_by_side(x):
        x = x.reshape(pairs, 2, context, HEAD_WIDTH)
        return jnp.concatenate([x[:, 0], x[:, 1]], axis=-1)

    q = q.reshape(both)
    q = jnp.concatenate([jnp.where(first, q, 0.0), jnp.where(first, 0.0, q)], axis=-1)
    scores = jnp.einsum(
        "phd,pcd->phc", q.astype(BF16), side_by_side(keys), preferred_element_type=F32
    )

    def mix(probs):
        mixed = jnp.einsum(
            "phc,pcd->phd", probs.reshape(pairs, 2 * heads, context), side_by_side(values),
            preferred_element_type=F32,
        )
        mixed = jnp.where(first, mixed[:, :, :HEAD_WIDTH], mixed[:, :, HEAD_WIDTH:])
        return mixed.reshape(chunk, heads, HEAD_WIDTH)

    return scores.reshape(chunk, heads, context), mix


def kernel(
    n_rep, n_tp, chunk, adapters, parts, early,
    len_hbm, q_hbm, kv_hbm, fresh_hbm, idx_hbm, table_hbm, down_hbm, w_hbm, up_hbm, res_hbm,
    out_ref,
    len_s, q_v, kv_v, fresh_v, idx_v, table_v, down_v, w_v, up_v, res_v,
    feat_v, part_send, part_recv, base_v, rs_send, rs_recv, ret_send, ret_recv,
    in_sem, kv_sem, w_sem, send_sem, share_sem, tag_sem, feat_sem, part_sem, rs_sem, ret_sem, far_sem,
):
    rep = lax.axis_index("rep")
    tp = lax.axis_index("tp")
    rows, width = q_v.shape
    heads = width // HEAD_WIDTH
    context = kv_v.shape[1]
    held = down_hbm.shape[0]
    joined = 2 * held
    rank = held // adapters
    out_width = up_v.shape[1]
    n_chip = n_rep // 2
    core = lax.rem(rep, 2)
    chip = lax.div(rep, 2)
    partner = rep + 1 - 2 * core

    def there(k):
        return {"rep": 2 * peer(chip, n_chip, k) + core}

    def back(k):
        return {"rep": 2 * source(chip, n_chip, k) + core}

    def along(k):
        return {"tp": peer(tp, n_tp, k)}

    relayed = n_tp == 4

    loads = {}
    for i, (name, src, dst) in enumerate((
        ("len", len_hbm, len_s), ("q", q_hbm, q_v), ("fresh", fresh_hbm, fresh_v),
        ("idx", idx_hbm, idx_v.at[0]), ("table", table_hbm, table_v),
        ("down", down_hbm, down_v.at[pl.ds(0, held)]), ("up", up_hbm, up_v.at[pl.ds(0, held)]),
        ("res", res_hbm, res_v),
    )):
        loads[name] = pltpu.make_async_copy(src, dst, in_sem.at[i])
    kv_loads = [
        pltpu.make_async_copy(
            kv_hbm.at[pl.ds(c, chunk)], kv_v.at[pl.ds(c, chunk)], kv_sem.at[c // chunk]
        )
        for c in range(0, rows, chunk)
    ]
    w_loads = []
    for k in range(n_tp):
        first = pl.multiple_of((peer(tp, n_tp, k) if k else tp) * out_width, out_width)
        w_loads.append(
            pltpu.make_async_copy(w_hbm.at[:, pl.ds(first, out_width)], w_v.at[k], w_sem.at[k])
        )

    barrier = pltpu.get_barrier_semaphore()
    greeted = [along(k) for k in ([1, 2] if relayed else range(1, n_tp))]
    greeted += [there(k) for k in range(1, n_chip)] + [{"rep": partner}]
    for device in greeted:
        pl.semaphore_signal(barrier, inc=1, device_id=device, device_id_type=MESH)
    for name in ("len", "q", "fresh"):
        loads[name].start()
    for copy in kv_loads:
        copy.start()
    for name in ("idx", "table"):
        loads[name].start()

    loads["len"].wait()
    loads["q"].wait()
    loads["fresh"].wait()
    scale = 1.0 / math.sqrt(HEAD_WIDTH)
    for c in range(0, rows, chunk):
        q = q_v[c : c + chunk, :].astype(F32).reshape(chunk, heads, HEAD_WIDTH)
        fresh = fresh_v[c : c + chunk, :].astype(F32).reshape(chunk, 1, 2 * HEAD_WIDTH)
        own = jnp.sum(q * fresh[:, :, :HEAD_WIDTH], axis=-1, keepdims=True) * scale
        live = jnp.concatenate(
            [iota((1, heads, context), 2) < len_s[c + i] for i in range(chunk)], axis=0
        )
        kv_loads[c // chunk].wait()
        if c == 0:
            for k in list(range(1, n_tp)) + [0]:
                w_loads[k].start()
            for name in ("down", "up", "res"):
                loads[name].start()
        kv = kv_v[c : c + chunk]
        scores, mix = attend(q, kv[:, :, :HEAD_WIDTH], kv[:, :, HEAD_WIDTH:])
        scores = jnp.where(live, scores * scale, -1e30)
        top = jnp.maximum(jnp.max(scores, axis=-1, keepdims=True), own)
        weights = jnp.where(live, jnp.exp(scores - top), 0.0)
        own_weight = jnp.exp(own - top)
        inverse = 1.0 / (jnp.sum(weights, axis=-1, keepdims=True) + own_weight)
        probs = (weights * inverse).astype(BF16)
        own_prob = (own_weight * inverse).astype(BF16).astype(F32)
        mixed = mix(probs) + own_prob * fresh[:, :, HEAD_WIDTH:]
        feat_v[0, c : c + chunk, :] = mixed.reshape(chunk, width).astype(BF16)

    pl.semaphore_wait(barrier, len(greeted))

    def send(kind, src, dst, recv_sem, device):
        pltpu.make_async_remote_copy(
            src_ref=src, dst_ref=dst, send_sem=send_sem.at[kind], recv_sem=recv_sem,
            device_id=device, device_id_type=MESH,
        ).start()

    def landed(ref, sem):
        pltpu.make_async_copy(ref, ref, sem).wait()

    TAGS, FEATURES, DOWN, UP, PARTS, SUMS, ANSWERS = range(7)
    others = pl.ds(1, n_chip - 1)
    for k in range(1, n_chip):
        send(TAGS, idx_hbm, idx_v.at[k], tag_sem, there(k))
    for i, part in enumerate(parts):
        for k, row, n in part:
            if k:
                span = pl.ds(row, n)
                send(FEATURES, feat_v.at[0, span], feat_v.at[k, span], feat_sem.at[i], there(k))
    send(DOWN, down_hbm, down_v.at[pl.ds(held, held)], share_sem.at[0], {"rep": partner})
    send(UP, up_hbm, up_v.at[pl.ds(held, held)], share_sem.at[1], {"rep": partner})
    if relayed:
        pl.semaphore_signal(far_sem, inc=1, device_id=along(1), device_id_type=MESH)

    tile = math.gcd(out_width, 256)

    def project(k):
        w_loads[k].wait()

        @pl.loop(0, out_width // tile)
        def _(j):
            columns = pl.ds(pl.multiple_of(j * tile, tile), tile)
            part = jnp.dot(feat_v[0], w_v[k, :, columns], preferred_element_type=F32)
            if k == 0:
                base_v[:, columns] = part
            else:
                rs_send[k, :, columns] = part.astype(BF16)

    def reduce(k):
        send(SUMS, rs_send.at[k], rs_recv.at[k], rs_sem, along(k))

    for k in range(1, n_tp):
        project(k)
        if k in early:
            reduce(k)

    loads["idx"].wait()
    loads["table"].wait()
    landed(idx_v.at[others], tag_sem)
    table_size = table_v.shape[1]
    places = []
    for k in range(n_chip):
        idx_col = as_column(idx_v[k], rows)
        slot_col = jnp.sum(
            jnp.where(iota((rows, table_size), 1) == idx_col, table_v[...], 0), axis=1, keepdims=True
        )
        owner_col = divide(slot_col, adapters)
        local_col = slot_col - owner_col * adapters
        places.append(
            jnp.where(
                owner_col == rep, local_col, jnp.where(owner_col == partner, local_col + adapters, -1)
            )
        )

    loads["down"].wait()
    landed(down_v.at[pl.ds(held, held)], share_sem.at[0])
    mines, sums, offset = [], [], 0
    for i, part in enumerate(parts):
        remote = [(k, row, n) for k, row, n in part if k]
        size = sum(n for _, _, n in part)
        half = size // 2
        landed(feat_v.at[pl.ds(1, len(remote)), pl.ds(0, remote[0][2])], feat_sem.at[i])
        features = jnp.concatenate([feat_v[k, row : row + n] for k, row, n in part], axis=0)
        products = lax.dot_general(
            features, down_v[...], (((1,), (1,)), ((), ())), preferred_element_type=F32
        )
        place = jnp.concatenate([places[k][row : row + n] for k, row, n in part], axis=0)
        mine = place == divide(iota((size, joined), 1), rank)
        masked = jnp.where(mine, products, 0.0)
        folded = masked[:, :LANES]
        for b in range(1, joined // LANES):
            folded = folded + masked[:, b * LANES : (b + 1) * LANES]
        folded = folded + pltpu.roll(folded, rank, 1)
        packed = jnp.where(iota((half, LANES), 1) < rank, folded[:half], folded[half:])
        span = pl.ds(offset, half)
        part_send[offset : offset + half, :] = packed.astype(BF16)
        if relayed and i == 0:
            pl.semaphore_wait(far_sem, 1)
        for k in reversed(range(1, n_tp)):
            send(PARTS, part_send.at[span], part_recv.at[k, span], part_sem.at[i], along(k))
        mines.append(mine)
        sums.append(packed)
        offset += half
    for k in range(1, n_tp):
        if k not in early:
            reduce(k)
    project(0)
    loads["res"].wait()
    base_v[...] += res_v[...].astype(F32)

    loads["up"].wait()
    landed(up_v.at[pl.ds(held, held)], share_sem.at[1])
    offset = 0
    for i, part in enumerate(parts):
        packed = sums[i]
        half = packed.shape[0]
        landed(part_recv.at[pl.ds(1, n_tp - 1), pl.ds(offset, half)], part_sem.at[i])
        for k in range(1, n_tp):
            packed = packed + part_recv[k, offset : offset + half, :].astype(F32)
        low = iota((half, LANES), 1) < rank
        rolled = pltpu.roll(packed, rank, 1)
        both = jnp.concatenate(
            [jnp.where(low, packed, rolled), jnp.where(low, rolled, packed)], axis=0
        )
        wide = jnp.concatenate([both] * (joined // LANES), axis=1)
        shrink = jnp.where(mines[i], wide, 0.0).astype(BF16)
        answers = jnp.dot(shrink, up_v[...], preferred_element_type=F32)
        at = 0
        for k, row, n in part:
            if k:
                ret_send[k, row : row + n, :] = answers[at : at + n].astype(BF16)
                span = pl.ds(row, n)
                send(ANSWERS, ret_send.at[k, span], ret_recv.at[k, span], ret_sem.at[i], back(k))
            else:
                base_v[row : row + n, :] += answers[at : at + n]
            at += n
        offset += half

    landed(rs_recv.at[pl.ds(1, n_tp - 1)], rs_sem)
    total = base_v[...]
    for k in range(1, n_tp):
        total = total + rs_recv[k].astype(F32)
    base_v[...] = total
    for i, part in enumerate(parts):
        remote = [(k, row, n) for k, row, n in part if k]
        landed(ret_recv.at[pl.ds(1, len(remote)), pl.ds(0, remote[0][2])], ret_sem.at[i])
        if i < len(parts) - 1:
            for k, row, n in remote:
                base_v[row : row + n, :] += ret_recv[k, row : row + n, :].astype(F32)
    for row in range(0, rows, chunk):
        total = base_v[row : row + chunk, :]
        for k, start, n in parts[-1]:
            if k and start <= row < start + n:
                total = total + ret_recv[k, row : row + chunk, :].astype(F32)
        out_ref[row : row + chunk, :] = total.astype(BF16)
    landed(idx_v.at[others], send_sem.at[TAGS])
    landed(feat_v.at[others], send_sem.at[FEATURES])
    landed(down_v.at[pl.ds(held, held)], send_sem.at[DOWN])
    landed(up_v.at[pl.ds(held, held)], send_sem.at[UP])
    landed(part_recv.at[pl.ds(1, n_tp - 1)], send_sem.at[PARTS])
    landed(rs_send.at[pl.ds(1, n_tp - 1)], send_sem.at[SUMS])
    landed(ret_send.at[others], send_sem.at[ANSWERS])


def on_device(
    n_rep, n_tp, queries, new_key_value, key_value_cache, lengths, residual, output_weight,
    row_adapter_index, adapter_storage_slot, adapter_down_weight, adapter_up_weight,
):
    rows, width = queries.shape
    context = key_value_cache.shape[2]
    adapters, _, rank = adapter_down_weight.shape
    out_width = adapter_up_weight.shape[2]
    table = adapter_storage_slot.shape[0]
    chunk = 16
    steps = rows // chunk
    n_chip = n_rep // 2
    joined = 2 * adapters * rank
    halves = n_chip * rows // 2
    assert n_rep % 2 == 0 and 2 * rank == LANES and joined % LANES == 0
    parts = [[(k, j * chunk, chunk) for k in range(n_chip)] for j in range(steps)]
    vmem = pltpu.VMEM
    dma = pltpu.SemaphoreType.DMA
    any_spec = pl.BlockSpec(memory_space=pltpu.HBM)
    return pl.pallas_call(
        functools.partial(kernel, n_rep, n_tp, chunk, adapters, parts, ()),
        out_shape=jax.ShapeDtypeStruct((rows, out_width), BF16),
        in_specs=[any_spec] * 10,
        out_specs=pl.BlockSpec(memory_space=pltpu.VMEM),
        scratch_shapes=[
            pltpu.SMEM((rows,), I32),
            vmem((rows, width), BF16),
            vmem((rows, context, 2 * HEAD_WIDTH), BF16),
            vmem((rows, 2 * HEAD_WIDTH), BF16),
            vmem((n_chip, 1, rows), I32),
            vmem((1, table), I32),
            vmem((joined, width), BF16),
            vmem((n_tp, width, out_width), BF16),
            vmem((joined, out_width), BF16),
            vmem((rows, out_width), BF16),
            vmem((n_chip, rows, width), BF16),
            vmem((halves, LANES), BF16),
            vmem((n_tp, halves, LANES), BF16),
            vmem((rows, out_width), F32),
            vmem((n_tp, rows, out_width), BF16),
            vmem((n_tp, rows, out_width), BF16),
            vmem((n_chip, rows, out_width), BF16),
            vmem((n_chip, rows, out_width), BF16),
            dma((8,)),
            dma((steps,)),
            dma((n_tp,)),
            dma((7,)),
            dma((2,)),
            dma,
            dma((len(parts),)),
            dma((len(parts),)),
            dma,
            dma((len(parts),)),
            pltpu.SemaphoreType.REGULAR,
        ],
        compiler_params=pltpu.CompilerParams(
            collective_id=0, has_side_effects=True, vmem_limit_bytes=24 * 1024 * 1024
        ),
        name="layer",
    )(*[
        pltpu.with_memory_space_constraint(a, pltpu.HBM)
        for a in (
            lengths, queries, key_value_cache.reshape(rows, context, 2 * HEAD_WIDTH),
            new_key_value.reshape(rows, 2 * HEAD_WIDTH), row_adapter_index.reshape(1, rows),
            adapter_storage_slot.reshape(1, table),
            jnp.swapaxes(adapter_down_weight, 1, 2).reshape(adapters * rank, width), output_weight,
            adapter_up_weight.reshape(adapters * rank, out_width), residual,
        )
    ])


def solution(mesh):
    in_specs = (
        P("rep", "tp"),
        P("rep", "tp", None),
        P("rep", "tp", None, None),
        P("rep"),
        P("rep", "tp"),
        P("tp", None),
        P("rep"),
        P(),
        P("rep", "tp", None),
        P("rep", None, "tp"),
    )
    return jax.shard_map(
        functools.partial(on_device, mesh.shape["rep"], mesh.shape["tp"]),
        mesh=mesh, in_specs=in_specs, out_specs=P("rep", "tp"), check_vma=False,
    )
```

time: 21.4 us -> 20.4 us (0.953)
  Pallas kernels: 20.6 us -> 19.6 us
    pallas_call x1, Pallas kernels: 20.6 us -> 19.6 us  [on_device(): pl.pallas_call(functools.partial(kernel, n_rep, n_tp, chunk, adapters, pa...]
where the time goes in v2:
time: 20.4 us; the launch traced here: 20.3 us
  Pallas kernels  19.6 us (96%)
  local copies, waits for them, and re-layouts  0.63 us (3%)
    pallas_call x1, Pallas kernels, on_device(): pl.pallas_call(functools.partial(kernel, n_rep, n_tp, chunk, adapters, pa...  19.6 us
    unnamed x1, local copies, waits for them, and re-layouts  0.63 us

profile of v2, /device:TPU:0, one launch (start us, length us, event | category | flops | bytes accessed | tf_op | source)
XLA Modules:
  0.0 20.3 jit_solution(5764238100411525259)
XLA Ops:
  0.0 19.6 %layer.1 = bf16[32,1024]{1,0:T(8,128)(2,1)S(1)} custom-call(s32[32]{0:T(128)} %len_hbm.1, bf16[32,1024]{1,0:T(8,128)(2,1)} %q_hbm.1, bf16[32,128,256]{2,1,0:T(8,128)(2,1)} %bitcast.8, bf16[32,256]{1,0:T(8,128)(2,1)} %bitcast.11, s32[1,32]{1,0:T(1,128)} %bitcast.12, s32[1,32]{1,0:T(1,128)} %bitcast.13, bf16[256,1024]{1,0:T(8,128)(2,1)} %bitcast.9, ...), custom_call_target="tpu_custom_call" | custom-call | tf_op jit(solution)/shard_map/layer/pallas_call | solution.py:345
  19.6 0.6 %copy.12 = bf16[32,1024]{1,0:T(8,128)(2,1)} copy(bf16[32,1024]{1,0:T(8,128)(2,1)S(1)} %layer.1) | data formatting | bytes 131072
